TPU v7x, 32 devices: a whole 2x2x4 slice. The times are simulated.
32 devices in a mesh: pa: 16 (over z, y, core), pb: 2 (over x).
Axes of the slice: x: 2, y: 2, z: 4, core: 2. Of those that a mesh axis runs over, the one named last changes fastest.
Arguments:
- sources: float32 [4096, 128], P(('pa', 'pb')), may hold values from -3 to 3, as said below
- targets: bfloat16 [4096, 128], P(('pa', 'pb')), may hold values from -2 to 2, as said below
- source_mass: float32 [4096], P(('pa', 'pb')), may hold values from -1 to 1
- target_mass: float32 [4096], P(('pa', 'pb')), may hold values from -1 to 1
Outputs:
- moved: float32 [4096, 128], P(('pa', 'pb'))
- dual_source: float32 [4096], P(('pa', 'pb'))
- dual_target: float32 [4096], P(('pa', 'pb'))
Inputs may be any that keep to these rules, and one draw needn't show every extreme that they name: `targets`: each block of 128 target rows is drawn around one cluster centre, a different one for each block. `sources`: each block of 128 source rows is drawn around a cluster centre of its own, drawn independently of the target centres, possibly offset by a common shift.
All inputs are finite; a program needn't handle non-finite values.
Results may differ from a plain program's by a relative error of at most 0.003.
Values may be sent and summed in bfloat16 or wider, within the bound.
A program may use at most 64 MiB of HBM per device.

v0:
```python
from functools import partial
import jax
import jax.numpy as jnp
from jax import lax
from jax.sharding import PartitionSpec as P

STEPS = 1
ITERS = 2
step_rate = 0.25
floor_value = -1e30


def merged(part, axis, combine):
    gathered = jax.tree.map(lambda a: lax.all_gather(a, axis), part)

    def take(source):
        return jax.tree.map(lambda a: lax.dynamic_index_in_dim(a, source, 0, False), gathered)

    return lax.fori_loop(
        1, lax.axis_size(axis), lambda source, state: combine(state, take(source)), take(0)
    )


def squares(coords):
    wide = coords.astype(jnp.float32)
    return jnp.sum(wide * wide, axis=1)


def pair_cost(left, left_norm, right, right_norm):
    inner = lax.dot_general(
        left, right, (((1,), (1,)), ((), ())), preferred_element_type=jnp.float32
    )
    return left_norm[:, None] + right_norm[None, :] - 2.0 * inner


def over_blocks(update, carry, total):
    block_width = 512 if total % 512 == 0 else total
    block_count = total // block_width
    if block_count == 1:
        return update(carry, 0, block_width)
    return lax.fori_loop(
        0,
        block_count,
        lambda position, current: update(current, position * block_width, block_width),
        carry,
    )


def lse_piece(rows, row_norm, columns, column_norm, carry, piece, start):

    def update(current, offset, length):
        chosen = lax.dynamic_slice_in_dim(columns, start + offset, length, 0)
        chosen_norm = lax.dynamic_slice_in_dim(column_norm, start + offset, length, 0)
        values = lax.dynamic_slice_in_dim(piece, offset, length, 0)
        scores = values[None, :] - pair_cost(rows, row_norm, chosen, chosen_norm)
        highest, totals = current
        raised = jnp.maximum(highest, jnp.max(scores, axis=1))
        totals = totals * jnp.exp(highest - raised) + jnp.sum(
            jnp.exp(scores - raised[:, None]), axis=1
        )
        return (raised, totals)

    return over_blocks(update, carry, piece.shape[0])


def plan_piece(rows, row_norm, row_pot, columns, column_norm, carry, piece, start):

    def update(current, offset, length):
        chosen = lax.dynamic_slice_in_dim(columns, start + offset, length, 0)
        chosen_norm = lax.dynamic_slice_in_dim(column_norm, start + offset, length, 0)
        values = lax.dynamic_slice_in_dim(piece, offset, length, 0)
        cost = pair_cost(rows, row_norm, chosen, chosen_norm)
        weights = jnp.exp(row_pot[:, None] + values[None, :] - cost).astype(jnp.bfloat16)
        return current + jnp.dot(weights, chosen, preferred_element_type=jnp.float32)

    return over_blocks(update, carry, piece.shape[0])


def join_lse(first, second):
    raised = jnp.maximum(first[0], second[0])
    return (raised, first[1] * jnp.exp(first[0] - raised) + second[1] * jnp.exp(second[0] - raised))


def start_lse(length):
    return (jnp.full((length,), floor_value, jnp.float32), jnp.zeros((length,), jnp.float32))


def finish(carry):
    return -(carry[0] + jnp.log(carry[1]))


def body(sources, targets, source_mass, target_mass):
    own_rows = sources.shape[0]
    own_targets = targets.shape[0]
    target_norm = squares(targets)
    moving = sources
    dual_target = jnp.zeros((own_targets,), jnp.float32)
    dual_source = jnp.zeros((own_rows,), jnp.float32)
    member = lax.axis_index("pb")
    half_targets = lax.all_gather(targets, "pa", axis=0, tiled=True)
    half_norm = squares(half_targets)
    pair_mass = lax.all_gather(source_mass, "pb", axis=0, tiled=True)
    pair_dual = jnp.zeros((pair_mass.shape[0],), jnp.float32)
    for flow_step in range(STEPS):
        coarse = moving.astype(jnp.bfloat16)
        pair_coarse = lax.all_gather(coarse, "pb", axis=0, tiled=True)
        pair_norm = squares(pair_coarse)
        pair_count = pair_coarse.shape[0]
        all_sources = lax.all_gather(pair_coarse, "pa", axis=0, tiled=True)
        all_source_norm = squares(all_sources)
        row_fold = partial(lse_piece, pair_coarse, pair_norm, half_targets, half_norm)
        column_fold = partial(lse_piece, targets, target_norm, all_sources, all_source_norm)
        shifted = dual_target + target_mass
        for sweep in range(ITERS + 1):
            shifted = dual_target + target_mass
            half_lse = row_fold(
                start_lse(pair_count),
                jax.tree.map(lambda part: lax.all_gather(part, "pa", axis=0, tiled=True), shifted),
                jnp.int32(0),
            )
            pair_dual = finish(merged((half_lse[0], half_lse[1]), "pb", join_lse))
            if sweep < ITERS:
                lifted = pair_dual + pair_mass
                dual_target = finish(
                    column_fold(
                        start_lse(own_targets),
                        jax.tree.map(
                            lambda part: lax.all_gather(part, "pa", axis=0, tiled=True), lifted
                        ),
                        jnp.int32(0),
                    )
                )
        plan_fold = partial(plan_piece, pair_coarse, pair_norm, pair_dual, half_targets, half_norm)
        empty = jnp.zeros((pair_count, sources.shape[1]), jnp.float32)
        pair_centre = plan_fold(
            empty,
            jax.tree.map(lambda part: lax.all_gather(part, "pa", axis=0, tiled=True), shifted),
            jnp.int32(0),
        )
        centre = lax.psum_scatter(
            pair_centre.astype(jnp.bfloat16), "pb", scatter_dimension=0, tiled=True
        ).astype(jnp.float32)
        moving = moving - 2.0 * step_rate * (moving - centre)
    dual_source = lax.dynamic_slice_in_dim(pair_dual, member * own_rows, own_rows, 0)
    return (moving, dual_source, dual_target)


def solution(mesh):
    return jax.shard_map(
        body,
        mesh=mesh,
        in_specs=(P(("pa", "pb"), None), P(("pa", "pb"), None), P(("pa", "pb")), P(("pa", "pb"))),
        out_specs=(P(("pa", "pb"), None), P(("pa", "pb")), P(("pa", "pb"))),
        check_vma=False,
    )
```

profile of v0, /device:TPU:0, one launch (start us, length us, event | category | flops | bytes accessed | tf_op | source)
XLA Modules:
  0.0 212.0 jit_solution(4313513718906820735)
XLA Ops:
  8.1 5.6 %all_gather.65 = bf16[256,128]{1,0:T(8,128)(2,1)} all-gather(bf16[128,128]{1,0:T(8,128)(2,1)S(1)} %convert_element_type.28), channel_id=1, replica_groups=mesh['pa'=16,'pb'=2] {'pb'}, dimensions={0}, use_global_device_ids=true | all-gather | bytes 98304 | tf_op jit(solution)/shard_map/all_gather | solution.py:106
  14.7 24.4 %all_gather.66 = bf16[2048,128]{1,0:T(8,128)(2,1)S(1)} all-gather(bf16[128,128]{1,0:T(8,128)(2,1)} %param.17), channel_id=1, replica_groups=mesh['pa'=16,'pb'=2] {'pa'}, dimensions={0}, use_global_device_ids=true | all-gather | bytes 557056 | tf_op jit(solution)/shard_map/all_gather | solution.py:100
  39.4 17.5 %all-gather.6 = f32[16,1,128]{2,1,0:T(1,128)S(1)} all-gather(f32[1,1,128]{2,1,0:T(1,128)S(1)} %bitcast.107), channel_id=1, replica_groups=mesh['pa'=16,'pb'=2] {'pa'}, dimensions={0}, use_global_device_ids=true | all-gather | bytes 8704 | tf_op jit(solution)/shard_map/all_gather | solution.py:118
  56.9 2.4 %while.112 = (s32[]{:T(128)}, f32[256]{0:T(256)S(1)}, f32[256]{0:T(256)S(1)}, f32[2048]{0:T(1024)S(1)}, f32[256]{0:T(256)S(1)}, /*index=5*/f32[2048]{0:T(1024)S(...) while((s32[]{:T(128)}, f32[256]{0:T(256)S(1)}, ...), condition=%wide.region_6.7_spmd.clone, body=%wide.region_3.6_spmd.clone.sunk | while | flops 34473220 | bytes 1271994 | solution.py:41
  59.4 4.2 %all-gather.9 = f32[2,1,128]{2,1,0:T(1,128)S(1)} all-gather(f32[1,1,128]{2,1,0:T(1,128)S(1)} %bitcast.124), channel_id=1, replica_groups=mesh['pa'=16,'pb'=2] {'pb'}, dimensions={0}, use_global_device_ids=true | all-gather | bytes 1536 | tf_op jit(solution)/shard_map/all_gather | solution.py:102
  63.7 4.2 %all-gather.7 = f32[2,1,256]{2,1,0:T(1,128)S(1)} all-gather(f32[1,1,256]{2,1,0:T(1,128)S(1)} %bitcast.98), channel_id=2, replica_groups=mesh['pa'=16,'pb'=2] {'pb'}, dimensions={0}, use_global_device_ids=true | all-gather | bytes 3072 | tf_op jit(solution)/shard_map/all_gather | solution.py:14
  67.9 4.2 %all-gather.8 = f32[2,1,256]{2,1,0:T(1,128)S(1)} all-gather(f32[1,1,256]{2,1,0:T(1,128)S(1)} %bitcast.106), channel_id=3, replica_groups=mesh['pa'=16,'pb'=2] {'pb'}, dimensions={0}, use_global_device_ids=true | all-gather | bytes 3072 | tf_op jit(solution)/shard_map/all_gather | solution.py:14
  72.2 18.8 %all-gather.10 = f32[16,1,256]{2,1,0:T(1,128)S(1)} all-gather(f32[1,1,256]{2,1,0:T(1,128)S(1)} %bitcast.113), channel_id=1, replica_groups=mesh['pa'=16,'pb'=2] {'pa'}, dimensions={0}, use_global_device_ids=true | all-gather | bytes 17408 | tf_op jit(solution)/shard_map/all_gather | solution.py:128
  91.2 1.8 multiply_reduce_fusion
  93.0 11.5 %while.113 = (s32[]{:T(128)}, f32[128]{0:T(128)S(1)}, f32[128]{0:T(128)S(1)}, f32[4096]{0:T(1024)S(1)}, f32[128]{0:T(128)S(1)}, /*index=5*/f32[4096]{0:T(1024)S(...) while((s32[]{:T(128)}, f32[128]{0:T(128)S(1)}, ...), condition=%wide.region_11.0_spmd.clone, body=%wide.region_8.11_spmd.clone.sunk | while | flops 17236612 | bytes 707770 | solution.py:41
  104.6 17.4 %all-gather.11 = f32[16,1,128]{2,1,0:T(1,128)S(1)} all-gather(f32[1,1,128]{2,1,0:T(1,128)S(1)} %add_bitcast_fusion.1), channel_id=1, replica_groups=mesh['pa'=16,'pb'=2] {'pa'}, dimensions={0}, use_global_device_ids=true | all-gather | bytes 8704 | tf_op jit(solution)/shard_map/all_gather | solution.py:118
  122.0 2.4 %while.114 = (s32[]{:T(128)}, f32[256]{0:T(256)S(1)}, f32[256]{0:T(256)S(1)}, f32[2048]{0:T(1024)S(1)}, f32[256]{0:T(256)S(1)}, /*index=5*/f32[2048]{0:T(1024)S(...) while((s32[]{:T(128)}, f32[256]{0:T(256)S(1)}, ...), condition=%wide.region_15.0_spmd.clone, body=%wide.region_12.15_spmd.clone.sunk | while | flops 34473220 | bytes 1271994 | solution.py:41
  124.4 4.2 %all-gather.12 = f32[2,1,256]{2,1,0:T(1,128)S(1)} all-gather(f32[1,1,256]{2,1,0:T(1,128)S(1)} %bitcast.97), channel_id=4, replica_groups=mesh['pa'=16,'pb'=2] {'pb'}, dimensions={0}, use_global_device_ids=true | all-gather | bytes 3072 | tf_op jit(solution)/shard_map/all_gather | solution.py:14
  128.7 4.2 %all-gather.13 = f32[2,1,256]{2,1,0:T(1,128)S(1)} all-gather(f32[1,1,256]{2,1,0:T(1,128)S(1)} %bitcast.105), channel_id=5, replica_groups=mesh['pa'=16,'pb'=2] {'pb'}, dimensions={0}, use_global_device_ids=true | all-gather | bytes 3072 | tf_op jit(solution)/shard_map/all_gather | solution.py:14
  132.9 18.8 %all-gather.14 = f32[16,1,256]{2,1,0:T(1,128)S(1)} all-gather(f32[1,1,256]{2,1,0:T(1,128)S(1)} %bitcast.112), channel_id=1, replica_groups=mesh['pa'=16,'pb'=2] {'pa'}, dimensions={0}, use_global_device_ids=true | all-gather | bytes 17408 | tf_op jit(solution)/shard_map/all_gather | solution.py:128
  151.7 11.5 %while.115 = (s32[]{:T(128)}, f32[128]{0:T(128)S(1)}, f32[128]{0:T(128)S(1)}, f32[4096]{0:T(1024)S(1)}, f32[128]{0:T(128)S(1)}, /*index=5*/f32[4096]{0:T(1024)S(...) while((s32[]{:T(128)}, f32[128]{0:T(128)S(1)}, ...), condition=%wide.region_19.20_spmd.clone, body=%wide.region_16.19_spmd.clone.sunk | while | flops 17236612 | bytes 707770 | solution.py:41
  160.5 1.1 fusion.116
  163.8 17.4 %all-gather.15 = f32[16,1,128]{2,1,0:T(1,128)S(1)} all-gather(f32[1,1,128]{2,1,0:T(1,128)S(1)} %get-tuple-element.1165), channel_id=1, replica_groups=mesh['pa'=16,'pb'=2] {'pa'}, dimensions={0}, use_global_device_ids=true | all-gather | bytes 8704 | tf_op jit(solution)/shard_map/all_gather | solution.py:137
  181.2 2.4 %while.116 = (s32[]{:T(128)}, f32[256]{0:T(256)S(1)}, f32[256]{0:T(256)S(1)}, f32[2048]{0:T(1024)S(1)}, f32[256]{0:T(256)S(1)}, /*index=5*/f32[2048]{0:T(1024)S(...) while((s32[]{:T(128)}, f32[256]{0:T(256)S(1)}, ...), condition=%wide.region_23.24_spmd.clone, body=%wide.region_20.23_spmd.clone.sunk | while | flops 34473220 | bytes 1271994 | solution.py:41
  183.6 4.2 %all-gather.16 = f32[2,1,256]{2,1,0:T(1,128)S(1)} all-gather(f32[1,1,256]{2,1,0:T(1,128)S(1)} %bitcast.96), channel_id=6, replica_groups=mesh['pa'=16,'pb'=2] {'pb'}, dimensions={0}, use_global_device_ids=true | all-gather | bytes 3072 | tf_op jit(solution)/shard_map/all_gather | solution.py:14
  187.9 4.2 %all-gather.17 = f32[2,1,256]{2,1,0:T(1,128)S(1)} all-gather(f32[1,1,256]{2,1,0:T(1,128)S(1)} %bitcast.104), channel_id=7, replica_groups=mesh['pa'=16,'pb'=2] {'pb'}, dimensions={0}, use_global_device_ids=true | all-gather | bytes 3072 | tf_op jit(solution)/shard_map/all_gather | solution.py:14
  192.1 2.4 %while.117 = (s32[]{:T(128)}, f32[256,128]{1,0:T(8,128)S(1)}, f32[256]{0:T(256)S(1)}, f32[2048]{0:T(1024)S(1)}, f32[256]{0:T(256)S(1)}, /*index=5*/f32[2048]{0:T...) while((s32[]{:T(128)}, f32[256,128]{1,0:T(8,128)S(1)}, ...), condition=%wide.region_25.0_spmd.clone, body=%wide.region_24.25_spmd.clone.sunk | while | flops 67960840 | bytes 605876 | solution.py:41
  195.8 8.0 %reduce-scatter.2.cloned.1.call-done = bf16[128,128]{1,0:T(8,128)(2,1)} async-done(((bf16[256,128]{1,0:T(8,128)(2,1)}), bf16[128,128]{1,0:T(8,128)(2,1)}) %reduce-scatter.2.cloned.1.call-update) | async-done | bytes 32784 | tf_op jit(solution)/shard_map/reduce_scatter | solution.py:140
  203.7 1.4 multiply_subtract_fusion
  (250 shorter events, 34.7 us)
Async XLA Ops:
  7.2 32.3 %copy-start.3 = (f32[128]{0:T(128)S(1)}, f32[128]{0:T(128)}, u32[]{:S(2)}) copy-start(f32[128]{0:T(128)} %param.19) | copy-start | bytes 1540
  7.2 84.0 %all-gather.20.cloned.1.call-start = ((), (), s32[]{:S(2)}) async-start(), calls=%async_computation.1 | async-start | bytes 1114112 | tf_op jit(solution)/shard_map/all_gather | solution.py:109
  13.7 43.2 %copy-start = (bf16[256,128]{1,0:T(8,128)(2,1)S(1)}, bf16[256,128]{1,0:T(8,128)(2,1)}, u32[]{:S(2)}) copy-start(bf16[256,128]{1,0:T(8,128)(2,1)} %all_gather.65) | copy-start | bytes 196612
  13.7 190.0 %reduce-scatter.2.cloned.1.call-start = ((), (), s32[]{:S(2)}) async-start(), calls=%async_computation.2 | async-start | bytes 98304 | tf_op jit(solution)/shard_map/reduce_scatter | solution.py:140
  56.9 2.5 %copy-start.4 = (f32[128]{0:T(128)S(1)}, f32[128]{0:T(128)}, u32[]{:S(2)}) copy-start(f32[128]{0:T(128)} %param.18) | copy-start | bytes 1540
  56.9 34.1 %copy-start.2 = (bf16[128,128]{1,0:T(8,128)(2,1)S(1)}, bf16[128,128]{1,0:T(8,128)(2,1)}, u32[]{:S(2)}) copy-start(bf16[128,128]{1,0:T(8,128)(2,1)} %param.17) | copy-start | bytes 98308
  192.1 11.6 %copy-start.1 = (f32[128,128]{1,0:T(8,128)S(1)}, f32[128,128]{1,0:T(8,128)}, u32[]{:S(2)}) copy-start(f32[128,128]{1,0:T(8,128)} %param.16) | copy-start | bytes 196612
Sparse Core Ops, SparseCore 0:
  13.8 40.4 all-gather.19
  195.3 8.3 reduce-scatter.1
where the time goes:
time: 213 us; the launch traced here: 212 us
  blocking collectives  150 us (70%)
  matrix products  23.1 us (11%)
  between operations  14.3 us (7%)
  other arithmetic  10.3 us (5%)
  waiting for transfers between devices  8.02 us (4%)
  local copies, waits for them, and re-layouts  5.52 us (3%)
    all_gather x5, blocking collectives, body(): lax.all_gather(part, 'pa', axis=0, tiled=True)  90 us
    all_gather x6, blocking collectives, merged(): gathered = jax.tree.map(lambda a: lax.all_gather(a, axis), part)  25.4 us
    all_gather x1, blocking collectives, body(): half_targets = lax.all_gather(targets, 'pa', axis=0, tiled=True)  24.4 us
    dot_general x28, matrix products, pair_cost(): lax.dot_general(left, right, (((1,), (1,)), ((), ())), preferred_element_...  21.5 us
    reduce_scatter x1, waiting for transfers between devices, body(): lax.psum_scatter(pair_centre.astype(jnp.bfloat16), 'pb', scatter_dimensio...  7.97 us
    all_gather x1, blocking collectives, body(): pair_coarse = lax.all_gather(coarse, 'pb', axis=0, tiled=True)  5.6 us
  transfers between devices with their start and end apart: 2, of which 1 were waited for; matrix products, arithmetic and copies ran while one was open for 2% of the time, Pallas kernels for 0%

commit v1 on v0

--- a/solution.py
+++ b/solution.py
@@ -97,7 +97,9 @@
     dual_target = jnp.zeros((own_targets,), jnp.float32)
     dual_source = jnp.zeros((own_rows,), jnp.float32)
     member = lax.axis_index("pb")
-    half_targets = lax.all_gather(targets, "pa", axis=0, tiled=True)
+    half_targets = jnp.concatenate(
+        lax.all_to_all(jnp.stack([targets] * lax.axis_size("pa")), "pa", 0, 0), axis=0
+    )
     half_norm = squares(half_targets)
     pair_mass = lax.all_gather(source_mass, "pb", axis=0, tiled=True)
     pair_dual = jnp.zeros((pair_mass.shape[0],), jnp.float32)

time: 213 us -> 203 us (0.953)
  blocking collectives: 150 us -> 129 us
  starting transfers between devices: 0.08 us -> 7.5 us
  matrix products: 23.1 us -> 26.5 us
    all_gather x1 -> x0, blocking collectives: 24.4 us -> none  [body(): half_targets = lax.all_gather(targets, 'pa', axis=0, tiled=True)]
    all_to_all x0 -> x1, starting transfers between devices: none -> 7.41 us  [body(): lax.all_to_all(jnp.stack([targets] * lax.axis_size('pa')), 'pa', 0, 0)]
    all_gather x5, blocking collectives: 90 us -> 94.2 us  [body(): lax.all_gather(part, 'pa', axis=0, tiled=True)]
    dot_general x28, matrix products: 21.5 us -> 24.9 us  [pair_cost(): lax.dot_general(left, right, (((1,), (1,)), ((), ())), preferred_element_...]
  transfers between devices with their start and end apart: 2 -> 3, of which waited for: 1 -> 1; matrix products, arithmetic and copies ran while one was open for 2% -> 4% of each run, Pallas kernels for 0% -> 0%
where the time goes in v1:
time: 203 us; the launch traced here: 202 us
  blocking collectives  129 us (64%)
  matrix products  26.5 us (13%)
  between operations  14.3 us (7%)
  other arithmetic  9.48 us (5%)
  starting transfers between devices  7.5 us (4%)
  local copies, waits for them, and re-layouts  7.23 us (4%)
  waiting for transfers between devices  6.86 us (3%)
    all_gather x5, blocking collectives, body(): lax.all_gather(part, 'pa', axis=0, tiled=True)  94.2 us
    all_gather x6, blocking collectives, merged(): gathered = jax.tree.map(lambda a: lax.all_gather(a, axis), part)  25.4 us
    dot_general x28, matrix products, pair_cost(): lax.dot_general(left, right, (((1,), (1,)), ((), ())), preferred_element_...  24.9 us
    all_to_all x1, starting transfers between devices, body(): lax.all_to_all(jnp.stack([targets] * lax.axis_size('pa')), 'pa', 0, 0)  7.41 us
    reduce_scatter x1, waiting for transfers between devices, body(): lax.psum_scatter(pair_centre.astype(jnp.bfloat16), 'pb', scatter_dimensio...  6.82 us
    all_gather x1, blocking collectives, body(): pair_coarse = lax.all_gather(coarse, 'pb', axis=0, tiled=True)  4.69 us
    all_gather x1, blocking collectives, body(): pair_mass = lax.all_gather(source_mass, 'pb', axis=0, tiled=True)  4.24 us
  transfers between devices with their start and end apart: 3, of which 1 were waited for; matrix products, arithmetic and copies ran while one was open for 4% of the time, Pallas kernels for 0%

profile of v1, /device:TPU:0, one launch (start us, length us, event | category | flops | bytes accessed | tf_op | source)
XLA Modules:
  0.0 201.5 jit_solution(14986865541327384486)
XLA Ops:
  7.2 1.7 stack.2
  8.9 7.4 %all-to-all-start = ((bf16[16,128,128]{2,1,0:T(8,128)(2,1)}), bf16[16,128,128]{2,1,0:T(8,128)(2,1)S(1)}, u32[]{:S(2)}, u32[]{:S(2)}) async-start(bf16[16,128,128]{2,1,0:T(8,128)(2,1)} %stack.2), calls=%async_computation | async-start | bytes 1048576 | tf_op jit(solution)/shard_map/all_to_all | solution.py:101
  16.4 4.7 %all_gather.62 = bf16[256,128]{1,0:T(8,128)(2,1)} all-gather(bf16[128,128]{1,0:T(8,128)(2,1)S(1)} %convert_element_type.29), channel_id=1, replica_groups=mesh['pa'=16,'pb'=2] {'pb'}, dimensions={0}, use_global_device_ids=true | all-gather | bytes 98304 | tf_op jit(solution)/shard_map/all_gather | solution.py:108
  21.3 4.2 %all-gather.9 = f32[2,1,128]{2,1,0:T(1,128)S(1)} all-gather(f32[1,1,128]{2,1,0:T(1,128)S(1)} %bitcast.128), channel_id=1, replica_groups=mesh['pa'=16,'pb'=2] {'pb'}, dimensions={0}, use_global_device_ids=true | all-gather | bytes 1536 | tf_op jit(solution)/shard_map/all_gather | solution.py:104
  25.5 21.7 %all-gather.6 = f32[16,1,128]{2,1,0:T(1,128)S(1)} all-gather(f32[1,1,128]{2,1,0:T(1,128)S(1)} %bitcast.111), channel_id=1, replica_groups=mesh['pa'=16,'pb'=2] {'pa'}, dimensions={0}, use_global_device_ids=true | all-gather | bytes 8704 | tf_op jit(solution)/shard_map/all_gather | solution.py:120
  48.7 5.8 %while.112 = (s32[]{:T(128)}, f32[256]{0:T(256)S(1)}, f32[256]{0:T(256)S(1)}, f32[2048]{0:T(1024)S(1)}, f32[256]{0:T(256)S(1)}, /*index=5*/f32[2048]{0:T(1024)S(...) while((s32[]{:T(128)}, f32[256]{0:T(256)S(1)}, ...), condition=%wide.region_6.7_spmd.clone, body=%wide.region_3.6_spmd.clone.sunk | while | flops 34473220 | bytes 1271994 | solution.py:41
  54.5 4.2 %all-gather.7 = f32[2,1,256]{2,1,0:T(1,128)S(1)} all-gather(f32[1,1,256]{2,1,0:T(1,128)S(1)} %bitcast.102), channel_id=2, replica_groups=mesh['pa'=16,'pb'=2] {'pb'}, dimensions={0}, use_global_device_ids=true | all-gather | bytes 3072 | tf_op jit(solution)/shard_map/all_gather | solution.py:14
  58.7 4.2 %all-gather.8 = f32[2,1,256]{2,1,0:T(1,128)S(1)} all-gather(f32[1,1,256]{2,1,0:T(1,128)S(1)} %bitcast.110), channel_id=3, replica_groups=mesh['pa'=16,'pb'=2] {'pb'}, dimensions={0}, use_global_device_ids=true | all-gather | bytes 3072 | tf_op jit(solution)/shard_map/all_gather | solution.py:14
  63.0 17.2 %all-gather.10 = f32[16,1,256]{2,1,0:T(1,128)S(1)} all-gather(f32[1,1,256]{2,1,0:T(1,128)S(1)} %bitcast.117), channel_id=1, replica_groups=mesh['pa'=16,'pb'=2] {'pa'}, dimensions={0}, use_global_device_ids=true | all-gather | bytes 17408 | tf_op jit(solution)/shard_map/all_gather | solution.py:130
  80.2 1.8 multiply_reduce_fusion
  82.0 11.5 %while.113 = (s32[]{:T(128)}, f32[128]{0:T(128)S(1)}, f32[128]{0:T(128)S(1)}, f32[4096]{0:T(1024)S(1)}, f32[128]{0:T(128)S(1)}, /*index=5*/f32[4096]{0:T(1024)S(...) while((s32[]{:T(128)}, f32[128]{0:T(128)S(1)}, ...), condition=%wide.region_11.0_spmd.clone, body=%wide.region_8.11_spmd.clone.sunk | while | flops 17236612 | bytes 707770 | solution.py:41
  93.6 19.1 %all-gather.11 = f32[16,1,128]{2,1,0:T(1,128)S(1)} all-gather(f32[1,1,128]{2,1,0:T(1,128)S(1)} %add_bitcast_fusion.1), channel_id=1, replica_groups=mesh['pa'=16,'pb'=2] {'pa'}, dimensions={0}, use_global_device_ids=true | all-gather | bytes 8704 | tf_op jit(solution)/shard_map/all_gather | solution.py:120
  112.7 2.4 %while.114 = (s32[]{:T(128)}, f32[256]{0:T(256)S(1)}, f32[256]{0:T(256)S(1)}, f32[2048]{0:T(1024)S(1)}, f32[256]{0:T(256)S(1)}, /*index=5*/f32[2048]{0:T(1024)S(...) while((s32[]{:T(128)}, f32[256]{0:T(256)S(1)}, ...), condition=%wide.region_15.0_spmd.clone, body=%wide.region_12.15_spmd.clone.sunk | while | flops 34473220 | bytes 1271994 | solution.py:41
  115.1 4.2 %all-gather.12 = f32[2,1,256]{2,1,0:T(1,128)S(1)} all-gather(f32[1,1,256]{2,1,0:T(1,128)S(1)} %bitcast.101), channel_id=4, replica_groups=mesh['pa'=16,'pb'=2] {'pb'}, dimensions={0}, use_global_device_ids=true | all-gather | bytes 3072 | tf_op jit(solution)/shard_map/all_gather | solution.py:14
  119.3 4.2 %all-gather.13 = f32[2,1,256]{2,1,0:T(1,128)S(1)} all-gather(f32[1,1,256]{2,1,0:T(1,128)S(1)} %bitcast.109), channel_id=5, replica_groups=mesh['pa'=16,'pb'=2] {'pb'}, dimensions={0}, use_global_device_ids=true | all-gather | bytes 3072 | tf_op jit(solution)/shard_map/all_gather | solution.py:14
  123.6 17.2 %all-gather.14 = f32[16,1,256]{2,1,0:T(1,128)S(1)} all-gather(f32[1,1,256]{2,1,0:T(1,128)S(1)} %bitcast.116), channel_id=1, replica_groups=mesh['pa'=16,'pb'=2] {'pa'}, dimensions={0}, use_global_device_ids=true | all-gather | bytes 17408 | tf_op jit(solution)/shard_map/all_gather | solution.py:130
  140.8 11.5 %while.115 = (s32[]{:T(128)}, f32[128]{0:T(128)S(1)}, f32[128]{0:T(128)S(1)}, f32[4096]{0:T(1024)S(1)}, f32[128]{0:T(128)S(1)}, /*index=5*/f32[4096]{0:T(1024)S(...) while((s32[]{:T(128)}, f32[128]{0:T(128)S(1)}, ...), condition=%wide.region_19.20_spmd.clone, body=%wide.region_16.19_spmd.clone.sunk | while | flops 17236612 | bytes 707770 | solution.py:41
  152.8 19.1 %all-gather.15 = f32[16,1,128]{2,1,0:T(1,128)S(1)} all-gather(f32[1,1,128]{2,1,0:T(1,128)S(1)} %get-tuple-element.1165), channel_id=1, replica_groups=mesh['pa'=16,'pb'=2] {'pa'}, dimensions={0}, use_global_device_ids=true | all-gather | bytes 8704 | tf_op jit(solution)/shard_map/all_gather | solution.py:139
  171.9 2.4 %while.116 = (s32[]{:T(128)}, f32[256]{0:T(256)S(1)}, f32[256]{0:T(256)S(1)}, f32[2048]{0:T(1024)S(1)}, f32[256]{0:T(256)S(1)}, /*index=5*/f32[2048]{0:T(1024)S(...) while((s32[]{:T(128)}, f32[256]{0:T(256)S(1)}, ...), condition=%wide.region_23.24_spmd.clone, body=%wide.region_20.23_spmd.clone.sunk | while | flops 34473220 | bytes 1271994 | solution.py:41
  174.3 4.2 %all-gather.16 = f32[2,1,256]{2,1,0:T(1,128)S(1)} all-gather(f32[1,1,256]{2,1,0:T(1,128)S(1)} %bitcast.100), channel_id=6, replica_groups=mesh['pa'=16,'pb'=2] {'pb'}, dimensions={0}, use_global_device_ids=true | all-gather | bytes 3072 | tf_op jit(solution)/shard_map/all_gather | solution.py:14
  178.5 4.2 %all-gather.17 = f32[2,1,256]{2,1,0:T(1,128)S(1)} all-gather(f32[1,1,256]{2,1,0:T(1,128)S(1)} %bitcast.108), channel_id=7, replica_groups=mesh['pa'=16,'pb'=2] {'pb'}, dimensions={0}, use_global_device_ids=true | all-gather | bytes 3072 | tf_op jit(solution)/shard_map/all_gather | solution.py:14
  182.8 2.4 %while.117 = (s32[]{:T(128)}, f32[256,128]{1,0:T(8,128)S(1)}, f32[256]{0:T(256)S(1)}, f32[2048]{0:T(1024)S(1)}, f32[256]{0:T(256)S(1)}, /*index=5*/f32[2048]{0:T...) while((s32[]{:T(128)}, f32[256,128]{1,0:T(8,128)S(1)}, ...), condition=%wide.region_25.0_spmd.clone, body=%wide.region_24.25_spmd.clone.sunk | while | flops 67960840 | bytes 605876 | solution.py:41
  186.4 6.8 %reduce-scatter.2.cloned.1.call-done = bf16[128,128]{1,0:T(8,128)(2,1)} async-done(((bf16[256,128]{1,0:T(8,128)(2,1)}), bf16[128,128]{1,0:T(8,128)(2,1)}) %reduce-scatter.2.cloned.1.call-update) | async-done | bytes 32784 | tf_op jit(solution)/shard_map/reduce_scatter | solution.py:142
  193.3 1.4 multiply_subtract_fusion
  (252 shorter events, 38.4 us)
Async XLA Ops:
  7.2 40.1 %copy-start.2 = (bf16[128,128]{1,0:T(8,128)(2,1)S(1)}, bf16[128,128]{1,0:T(8,128)(2,1)}, u32[]{:S(2)}) copy-start(bf16[128,128]{1,0:T(8,128)(2,1)} %param.17) | copy-start | bytes 98308
  7.2 9.2 %copy-start.1 = (f32[128,128]{1,0:T(8,128)S(1)}, f32[128,128]{1,0:T(8,128)}, u32[]{:S(2)}) copy-start(f32[128,128]{1,0:T(8,128)} %param.16) | copy-start | bytes 196612
  7.2 14.1 %copy-start.4 = (f32[128]{0:T(128)S(1)}, f32[128]{0:T(128)}, u32[]{:S(2)}) copy-start(f32[128]{0:T(128)} %param.18) | copy-start | bytes 1540
  7.2 18.3 %copy-start.3 = (f32[128]{0:T(128)S(1)}, f32[128]{0:T(128)}, u32[]{:S(2)}) copy-start(f32[128]{0:T(128)} %param.19) | copy-start | bytes 1540
  8.9 39.4 %all-to-all-start = ((bf16[16,128,128]{2,1,0:T(8,128)(2,1)}), bf16[16,128,128]{2,1,0:T(8,128)(2,1)S(1)}, u32[]{:S(2)}, u32[]{:S(2)}) async-start(bf16[16,128,128]{2,1,0:T(8,128)(2,1)} %stack.2), calls=%async_computation | async-start | bytes 1048576 | tf_op jit(solution)/shard_map/all_to_all | solution.py:101
  16.3 63.8 %all-gather.20.cloned.1.call-start = ((), (), s32[]{:S(2)}) async-start(), calls=%async_computation.2 | async-start | bytes 1114112 | tf_op jit(solution)/shard_map/all_gather | solution.py:111
  21.1 172.1 %reduce-scatter.2.cloned.1.call-start = ((), (), s32[]{:S(2)}) async-start(), calls=%async_computation.3 | async-start | bytes 98304 | tf_op jit(solution)/shard_map/reduce_scatter | solution.py:142
  82.0 30.7 %copy-start = (bf16[256,128]{1,0:T(8,128)(2,1)S(1)}, bf16[256,128]{1,0:T(8,128)(2,1)}, u32[]{:S(2)}) copy-start(bf16[256,128]{1,0:T(8,128)(2,1)} %get-tuple-element.1729) | copy-start | bytes 196612
Sparse Core Ops, SparseCore 0:
  21.3 39.1 all-gather.19
  186.0 7.2 reduce-scatter.1
